TPU v7x, 32 devices: a whole 2x2x4 slice. The times are simulated.
32 devices in a mesh: grp: 2 (over y), tp: 8 (over z, x), sub: 2 (over core).
Axes of the slice: x: 2, y: 2, z: 4, core: 2. Of those that a mesh axis runs over, the one named last changes fastest.
Arguments:
- hidden_in: bfloat16 [32, 2, 4096], P('grp', 'sub', 'tp'), parts along dimension 0, may hold values from -16 to 16
- norm_attn: float32 [8192], replicated, may hold values from 0.25 to 1.75
- w_query: bfloat16 [8192, 2, 4096], P(None, 'sub', 'tp'), may hold values from -0.0625 to 0.0625
- w_key: bfloat16 [8192, 2, 512], P(None, 'sub', 'tp'), may hold values from -0.0625 to 0.0625
- w_value: bfloat16 [8192, 2, 512], P(None, 'sub', 'tp'), may hold values from -0.0625 to 0.0625
- w_out: bfloat16 [2, 4096, 2, 4096], P('sub', None, None, 'tp'), may hold values from -0.0625 to 0.0625
- norm_ffn: float32 [8192], replicated, may hold values from 0.25 to 1.75
- w_gate: bfloat16 [2, 4096, 14336], P('sub', None, 'tp'), may hold values from -0.0625 to 0.0625
- w_up: bfloat16 [2, 4096, 14336], P('sub', None, 'tp'), may hold values from -0.0625 to 0.0625
- w_down: bfloat16 [14336, 2, 4096], P('tp', 'sub'), may hold values from -0.0625 to 0.0625
- cache_keys: bfloat16 [32, 64, 8, 128], P('grp', 'tp', 'sub'), parts along dimension 0, may hold values from -250 to 250
- cache_values: bfloat16 [32, 64, 8, 128], P('grp', 'tp', 'sub'), parts along dimension 0, may hold values from -6 to 6
- lengths: int32 [32], P('grp'), parts along dimension 0, may hold values from 1 to 64, as said below
Outputs:
- hidden_out: bfloat16 [32, 2, 4096], P('grp', 'sub', 'tp'), parts along dimension 0
There are 2 independent parts, one for each index of `grp`. A program takes and returns all parts, laid end to end along the dimension named above; an argument that names none is the same for every part. Nothing has to cross between parts.
Inputs may be any that keep to these rules, and one draw needn't show every extreme that they name: `lengths`: some sequence has 64 live positions and some has 1.
All inputs are finite; a program needn't handle non-finite values.
Results may differ from a plain program's by a relative error of at most 0.012.
The roundings to bfloat16 on the way count: a program that leaves them out, or rounds other values in their place, can miss the bound.
Values may be sent and summed in bfloat16 or wider, within the bound.
A program may use at most 128 MiB of HBM per device.

v0:
```python
import math
import jax
import jax.numpy as jnp
from jax import lax
from jax.sharding import PartitionSpec as P

HD = 128
epsilon = 1e-05
rope_base = 500000.0
floor_score = -1e30


def joined(part, axis, combine):
    gathered = jax.tree.map(lambda a: lax.all_gather(a, axis), part)

    def take(source):
        return jax.tree.map(lambda a: lax.dynamic_index_in_dim(a, source, 0, False), gathered)

    return lax.fori_loop(
        1, lax.axis_size(axis), lambda source, state: combine(state, take(source)), take(0)
    )


def rope_angles(lengths):
    frequencies = rope_base ** (-(jnp.arange(HD // 2, dtype=jnp.float32) * 2.0) / HD)
    return lengths.astype(jnp.float32)[:, None] * frequencies[None, :]


def rotate(vectors, angles):
    middle_index = vectors.shape[-1] // 2
    cosine = jnp.cos(angles)[:, None, :]
    sine = jnp.sin(angles)[:, None, :]
    lower = vectors[..., :middle_index]
    upper = vectors[..., middle_index:]
    return jnp.concatenate([lower * cosine - upper * sine, upper * cosine + lower * sine], axis=-1)


def spread_rows(shard):
    across = lax.all_gather(shard, "tp", axis=2, tiled=True)
    return lax.all_gather(across, "sub", axis=1, tiled=True)


def half_rows_of(shard):
    return lax.all_gather(shard, "tp", axis=2, tiled=True)


def join_partials(earlier, later):
    earlier_max, earlier_sum, earlier_out = earlier
    later_max, later_sum, later_out = later
    highest = jnp.maximum(earlier_max, later_max)
    earlier_scale = jnp.exp(earlier_max - highest)
    later_scale = jnp.exp(later_max - highest)
    joined_sum = earlier_sum * earlier_scale + later_sum * later_scale
    joined_out = earlier_out * earlier_scale[..., None] + later_out * later_scale[..., None]
    return (highest, joined_sum, joined_out)


def per_device(
    hidden_in,
    norm_attn,
    w_query,
    w_key,
    w_value,
    w_out,
    norm_ffn,
    w_gate,
    w_up,
    w_down,
    cache_keys,
    cache_values,
    lengths,
):
    seq_count = hidden_in.shape[0]
    shard_width = hidden_in.shape[2]
    half_width = shard_width * lax.axis_size("tp")
    model_width = half_width * lax.axis_size("sub")
    tp_pos = lax.axis_index("tp")
    sub_pos = lax.axis_index("sub")
    residual = hidden_in.astype(jnp.float32)
    whole_rows = spread_rows(hidden_in).astype(jnp.float32)
    factor = lax.rsqrt(jnp.mean(whole_rows * whole_rows, axis=(1, 2)) + epsilon)
    gain_whole = norm_attn.reshape(whole_rows.shape[1], half_width)
    gathered = (whole_rows * factor[:, None, None] * gain_whole).astype(jnp.bfloat16)
    flattened = gathered.reshape(seq_count, model_width)
    query_part = jnp.dot(
        flattened, w_query.reshape(model_width, -1), preferred_element_type=jnp.float32
    ).astype(jnp.bfloat16)
    key_part = jnp.dot(
        flattened, w_key.reshape(model_width, -1), preferred_element_type=jnp.float32
    ).astype(jnp.bfloat16)
    value_part = jnp.dot(
        flattened, w_value.reshape(model_width, -1), preferred_element_type=jnp.float32
    ).astype(jnp.bfloat16)
    query, key_new, value_new = (
        lax.all_gather(query_part, "tp", axis=1, tiled=True),
        lax.all_gather(key_part, "tp", axis=1, tiled=True),
        lax.all_gather(value_part, "tp", axis=1, tiled=True),
    )
    query_heads = query.shape[1] // HD
    kv_heads = key_new.shape[1] // HD
    group_size = query_heads // kv_heads
    angles = rope_angles(lengths)
    query_rot = rotate(
        query.astype(jnp.float32).reshape(seq_count, query_heads, HD), angles
    ).astype(jnp.bfloat16)
    key_rot = rotate(key_new.astype(jnp.float32).reshape(seq_count, kv_heads, HD), angles).astype(
        jnp.bfloat16
    )
    grouped = query_rot.reshape(seq_count, kv_heads, group_size, HD)
    values_new = value_new.astype(jnp.float32).reshape(seq_count, kv_heads, 1, HD)
    span = cache_keys.shape[1]
    scores = jnp.einsum(
        "bkgd,blkd->bkgl", grouped, cache_keys, preferred_element_type=jnp.float32
    ) / math.sqrt(HD)
    places = tp_pos * span + jnp.arange(span, dtype=jnp.int32)
    live = (places[None, :] < lengths[:, None])[:, None, None, :]
    masked = jnp.where(live, scores, floor_score)
    local_max = jnp.max(masked, axis=-1)
    weights = jnp.where(live, jnp.exp(masked - local_max[..., None]), 0.0)
    local_sum = jnp.sum(weights, axis=-1)
    local_out = jnp.einsum(
        "bkgl,blkd->bkgd",
        weights,
        cache_values.astype(jnp.float32),
        precision=lax.Precision.HIGHEST,
    )
    own_score = jnp.sum(
        grouped.astype(jnp.float32) * key_rot.astype(jnp.float32)[:, :, None, :], axis=-1
    ) / math.sqrt(HD)
    joined_max, joined_sum, joined_out = joined(
        (local_max, local_sum, local_out), "tp", join_partials
    )
    highest = jnp.maximum(joined_max, own_score)
    kept_scale = jnp.exp(joined_max - highest)
    own_weight = jnp.exp(own_score - highest)
    numerator = joined_out * kept_scale[..., None] + own_weight[..., None] * values_new
    denominator = joined_sum * kept_scale + own_weight
    attended = (numerator / denominator[..., None]).reshape(seq_count, -1).astype(jnp.bfloat16)
    out_part = jnp.dot(
        attended, w_out.reshape(attended.shape[1], -1), preferred_element_type=jnp.float32
    )
    out_part = out_part.reshape(seq_count, -1, shard_width)
    mixed = lax.psum_scatter(out_part, "sub", scatter_dimension=1, tiled=True)
    middle = (residual + mixed).astype(jnp.bfloat16)
    middle_float = middle.astype(jnp.float32)
    raw_half = half_rows_of(middle).astype(jnp.float32)
    partial_squares = jnp.sum(raw_half * raw_half, axis=(1, 2))
    squares_mid = lax.psum(partial_squares, "sub")
    factor_mid = lax.rsqrt(squares_mid / model_width + epsilon)
    gain_half = lax.dynamic_slice_in_dim(norm_ffn, sub_pos * half_width, half_width)
    half_rows = (raw_half * factor_mid[:, None, None] * gain_half).astype(jnp.bfloat16)
    half_flat = half_rows.reshape(seq_count, half_width)
    gate_part = jnp.dot(
        half_flat, w_gate.reshape(half_width, -1), preferred_element_type=jnp.float32
    )
    up_part = jnp.dot(half_flat, w_up.reshape(half_width, -1), preferred_element_type=jnp.float32)
    gate_total, up_total = lax.psum((gate_part, up_part), "sub")
    hidden = (jax.nn.silu(gate_total) * up_total).astype(jnp.bfloat16)
    down_part = jnp.dot(
        hidden, w_down.reshape(hidden.shape[1], -1), preferred_element_type=jnp.float32
    )
    down_total = lax.psum(down_part, "tp")
    down_share = lax.dynamic_slice_in_dim(down_total, tp_pos * shard_width, shard_width, 1)
    return (middle_float + down_share[:, None, :]).astype(jnp.bfloat16)


def solution(mesh):
    in_specs = (
        P("grp", "sub", "tp"),
        P(),
        P(None, "sub", "tp"),
        P(None, "sub", "tp"),
        P(None, "sub", "tp"),
        P("sub", None, None, "tp"),
        P(),
        P("sub", None, "tp"),
        P("sub", None, "tp"),
        P("tp", "sub", None),
        P("grp", "tp", "sub", None),
        P("grp", "tp", "sub", None),
        P("grp"),
    )
    out_specs = P("grp", "sub", "tp")
    return jax.shard_map(
        per_device, mesh=mesh, in_specs=in_specs, out_specs=out_specs, check_vma=False
    )
```

profile of v0, /device:TPU:0, one launch (start us, length us, event | category | flops | bytes accessed | tf_op | source)
XLA Modules:
  0.0 410.7 jit_solution(6426538400944346462)
XLA Ops:
  6.6 32.7 %all_gather.36 = bf16[16,1,4096]{2,0,1:T(8,128)(2,1)S(1)} all-gather(bf16[16,1,512]{2,0,1:T(8,128)(2,1)} %param.15), channel_id=1, replica_groups=mesh['grp'=2,'tp'=8,'sub'=2] {'tp'}, dimensions={2}, use_global_device_ids=true | all-gather | bytes 147456 | tf_op jit(solution)/shard_map/all_gather | solution.py:39
  39.3 2.0 all_gather.37
  41.3 0.2 fusion.19
  41.5 0.8 mul.255
  42.3 0.1 fusion.25
  42.4 4.6 %fusion.12 = bf16[16,512]{1,0:T(8,128)(2,1)S(1)} fusion(bf16[16,8192]{1,0:T(8,128)(2,1)S(1)} %bitcast.90, bf16[8192,1,512]{2,0,1:T(8,128)(2,1)} %param.17), kind=kOutput, calls=%fused_computation.18 | convolution fusion | flops 134225920 | bytes 8667136 | tf_op jit(solution)/shard_map/dot_general | solution.py:85
  47.0 30.5 %all_gather.38 = bf16[16,4096]{1,0:T(8,128)(2,1)S(1)} all-gather(bf16[16,512]{1,0:T(8,128)(2,1)S(1)} %fusion.12), channel_id=1, replica_groups=mesh['grp'=2,'tp'=8,'sub'=2] {'tp'}, dimensions={1}, use_global_device_ids=true | all-gather | bytes 147456 | tf_op jit(solution)/shard_map/all_gather | solution.py:95
  77.7 0.1 multiply_cosine_fusion
  77.8 0.1 fusion.28
  78.0 0.3 fusion.48
  78.3 1.3 fusion.26
  79.7 0.2 fusion.27
  79.9 31.0 %all-gather.1 = f32[128,4,8]{2,1,0:T(4,128)S(1)} all-gather(f32[16,4,8]{2,1,0:T(4,128)S(1)} %fusion.27), channel_id=3, replica_groups=mesh['grp'=2,'tp'=8,'sub'=2] {'tp'}, dimensions={0}, use_global_device_ids=true | all-gather | bytes 18432 | tf_op jit(solution)/shard_map/all_gather | solution.py:14
  110.9 0.1 copy.68
  111.0 0.1 copy.66
  111.1 31.7 %all-gather = f32[128,4,8]{2,1,0:T(4,128)S(1)} all-gather(f32[16,4,8]{2,1,0:T(4,128)S(1)} %get-tuple-element.236), channel_id=2, replica_groups=mesh['grp'=2,'tp'=8,'sub'=2] {'tp'}, dimensions={0}, use_global_device_ids=true | all-gather | bytes 18432 | tf_op jit(solution)/shard_map/all_gather | solution.py:14
  142.8 0.1 copy.67
  142.9 0.1 copy.65
  143.0 0.4 fusion.15
  143.4 30.6 %all-gather.3 = bf16[8,64,16]{1,2,0:T(8,128)(2,1)S(1)} all-gather(bf16[1,64,16]{1,2,0:T(8,128)(2,1)S(1)} %fusion.15), channel_id=1, replica_groups=mesh['grp'=2,'tp'=8,'sub'=2] {'tp'}, dimensions={0}, use_global_device_ids=true | all-gather | bytes 18432 | tf_op jit(solution)/shard_map/all_gather | solution.py:96
  174.2 0.1 subtract_convert_fusion.1
  174.3 0.3 multiply_reduce_fusion
  174.7 0.4 fusion.16
  175.1 30.6 %all-gather.4 = bf16[8,64,16]{1,2,0:T(8,128)(2,1)S(1)} all-gather(bf16[1,64,16]{1,2,0:T(8,128)(2,1)S(1)} %fusion.16), channel_id=1, replica_groups=mesh['grp'=2,'tp'=8,'sub'=2] {'tp'}, dimensions={0}, use_global_device_ids=true | all-gather | bytes 18432 | tf_op jit(solution)/shard_map/all_gather | solution.py:97
  205.8 9.3 %copy.83 = bf16[512,8,2,512]{3,1,2,0:T(8,128)(2,1)} copy(bf16[512,8,2,512]{3,2,1,0:T(2,128)(2,1)} %bitcast.89) | data formatting | bytes 16777216
  215.1 11.4 %copy.75 = bf16[1024,4096]{1,0:T(8,128)(2,1)} copy(bf16[1024,4096]{0,1:T(8,128)(2,1)} %bitcast.88) | data formatting | bytes 16777216 | tf_op jit(solution)/shard_map/dot_general | solution.py:139
  226.5 1.0 slice.26
  227.5 10.0 %while.19 = (s32[]{:T(128)}, f32[16,4,8]{0,2,1:T(8,128)S(1)}, f32[16,4,8]{0,2,1:T(8,128)S(1)}, f32[16,4,8,128]{3,2,1,0:T(8,128)S(1)}, f32[8,16,4,8]{1,3,2,0:T(8,...) while((s32[]{:T(128)}, f32[16,4,8]{0,2,1:T(8,128)S(1)}, ...), condition=%wide.region_4.5_spmd, body=%wide.region_3.4_spmd.sunk | while | flops 199685 | bytes 815255 | solution.py:19
  227.7 1.2 fusion.58
  229.1 1.2 fusion.58
  230.5 1.2 fusion.58
  231.9 1.2 fusion.58
  233.4 1.2 fusion.58
  234.8 1.2 fusion.58
  236.2 1.2 fusion.58
  237.7 0.3 divide_convert_fusion
  238.1 6.3 %fusion.49 = f32[16,2,512]{2,0,1:T(8,128)} fusion(bf16[16,4096,1]{1,0,2:T(8,128)(2,1)S(1)} %reshape.198, bf16[2,512,4096]{2,1,0:T(8,128)(2,1)} %bitcast.87), kind=kOutput, calls=%fused_computation.77 | convolution fusion | flops 134217728 | bytes 8585216 | tf_op jit(solution)/shard_map/dot_general | solution.py:139
  244.5 8.5 %reduce-scatter.2.cloned.1.call-done = f32[16,1,512]{2,0,1:T(8,128)} async-done(((f32[16,2,512]{2,0,1:T(8,128)}), f32[16,1,512]{2,0,1:T(8,128)}) %reduce-scatter.2.cloned.1.call-update) | async-done | bytes 32784 | tf_op jit(solution)/shard_map/reduce_scatter | solution.py:143
  253.0 0.8 add_convert_fusion.1
  253.8 30.8 %all_gather.47 = bf16[16,1,4096]{2,0,1:T(8,128)(2,1)S(1)} all-gather(bf16[16,1,512]{2,0,1:T(8,128)(2,1)S(1)} %add_convert_fusion.1), channel_id=1, replica_groups=mesh['grp'=2,'tp'=8,'sub'=2] {'tp'}, dimensions={2}, use_global_device_ids=true | all-gather | bytes 147456 | tf_op jit(solution)/shard_map/all_gather | solution.py:44
  284.5 0.1 fusion.22
  284.7 2.6 psum.28
  287.3 7.9 %fusion.7 = f32[16,1792]{1,0:T(8,128)} fusion(bf16[1,4096,1792]{2,1,0:T(8,128)(2,1)} %param.22, bf16[16,1,4096]{2,0,1:T(8,128)(2,1)S(1)} %all_gather.47, f32[4096]{0:T(1024)S(1)} %dynamic_slice.50, f32[16]{0:T(128)S(1)} %add_rsqrt_fusion), kind=kOutput, calls=%fused_computation.12 | convolution fusion | flops 235143168 | bytes 14942272 | tf_op jit(solution)/shard_map/dot_general | solution.py:153
  295.2 7.9 %fusion.5 = f32[16,1792]{1,0:T(8,128)} fusion(bf16[1,4096,1792]{2,1,0:T(8,128)(2,1)} %param.23, bf16[16,1,4096]{2,0,1:T(8,128)(2,1)S(1)} %all_gather.47, f32[4096]{0:T(1024)S(1)} %dynamic_slice.50, f32[16]{0:T(128)S(1)} %add_rsqrt_fusion), kind=kOutput, calls=%fused_computation.10 | convolution fusion | flops 235143168 | bytes 14942272 | tf_op jit(solution)/shard_map/dot_general | solution.py:156
  303.2 19.1 %all-reduce.6.cloned.1.call-done = (f32[16,1792]{1,0:T(8,128)}, f32[16,1792]{1,0:T(8,128)}) async-done(((f32[16,1792]{1,0:T(8,128)}, f32[16,1792]{1,0:T(8,128)}), (f32[16,1792]{1,0:T(8,128)}, f32[16,1792]{1,0:T(8,128)})) %all-reduce.6.cloned.1.call-update) | async-done | bytes 229392 | tf_op jit(solution)/shard_map/psum | solution.py:157
  322.4 8.0 %fusion.3 = f32[16,4096]{1,0:T(8,128)} fusion(bf16[1792,1,4096]{2,0,1:T(8,128)(2,1)} %param.24, f32[16,1792]{1,0:T(8,128)} %get-tuple-element.221, f32[16,1792]{1,0:T(8,128)} %get-tuple-element.222), kind=kOutput, calls=%fused_computation.8 | convolution fusion | flops 235053056 | bytes 15171584 | tf_op jit(solution)/shard_map/dot_general | solution.py:159
  330.4 72.4 %all-reduce.4.cloned.1.call-done = f32[16,4096]{1,0:T(8,128)} async-done(((f32[16,4096]{1,0:T(8,128)}), f32[16,4096]{1,0:T(8,128)}) %all-reduce.4.cloned.1.call-update) | async-done | bytes 262160 | tf_op jit(solution)/shard_map/psum | solution.py:162
  402.8 1.4 fusion.37
  (71 shorter events, 2.4 us)
Async XLA Ops:
  6.5 136.5 %copy-start = (bf16[8192,1,64]{0,2,1:T(8,128)(2,1)S(1)}, bf16[8192,1,64]{0,2,1:T(8,128)(2,1)}, u32[]{:S(2)}) copy-start(bf16[8192,1,64]{0,2,1:T(8,128)(2,1)} %param.18) | copy-start | bytes 3145732
  6.5 71.1 %copy-start.7 = (s32[16]{0:T(128)S(1)}, s32[16]{0:T(128)}, u32[]{:S(2)}) copy-start(s32[16]{0:T(128)} %param.27) | copy-start | bytes 196
  6.5 71.4 %copy-start.3 = (bf16[16,8,4,128]{3,2,1,0:T(4,128)(2,1)S(1)}, bf16[16,8,4,128]{3,2,1,0:T(4,128)(2,1)}, u32[]{:S(2)}) copy-start(bf16[16,8,4,128]{3,2,1,0:T(4,128)(2,1)} %param.25) | copy-start | bytes 393220
  6.5 71.8 %copy-start.4 = (bf16[16,8,4,128]{3,2,1,0:T(4,128)(2,1)S(1)}, bf16[16,8,4,128]{3,2,1,0:T(4,128)(2,1)}, u32[]{:S(2)}) copy-start(bf16[16,8,4,128]{3,2,1,0:T(4,128)(2,1)} %param.26) | copy-start | bytes 393220
  6.5 168.1 %copy-start.2 = (bf16[8192,1,64]{0,2,1:T(8,128)(2,1)S(1)}, bf16[8192,1,64]{0,2,1:T(8,128)(2,1)}, u32[]{:S(2)}) copy-start(bf16[8192,1,64]{0,2,1:T(8,128)(2,1)} %param.19) | copy-start | bytes 3145732
  6.5 219.9 %all-gather.7.cloned.1.call-start = ((), (), s32[]{:S(2)}) async-start(), calls=%async_computation.3 | async-start | bytes 2359296 | tf_op jit(solution)/shard_map/all_gather | solution.py:14
  79.7 173.3 %reduce-scatter.2.cloned.1.call-start = ((), (), s32[]{:S(2)}) async-start(), calls=%async_computation.1 | async-start | bytes 98304 | tf_op jit(solution)/shard_map/reduce_scatter | solution.py:143
  215.1 29.3 %copy-start.6 = (f32[8192]{0:T(1024)S(1)}, f32[8192]{0:T(1024)}, u32[]{:S(2)}) copy-start(f32[8192]{0:T(1024)} %param.21) | copy-start | bytes 98308
  215.1 37.9 %copy-start.5 = (bf16[16,1,512]{2,0,1:T(8,128)(2,1)S(1)}, bf16[16,1,512]{2,0,1:T(8,128)(2,1)}, u32[]{:S(2)}) copy-start(bf16[16,1,512]{2,0,1:T(8,128)(2,1)} %param.15) | copy-start | bytes 49156
  244.4 78.0 %all-reduce.6.cloned.1.call-start = ((), (), s32[]{:S(2)}) async-start(), calls=%async_computation.4 | async-start | bytes 458752 | tf_op jit(solution)/shard_map/psum | solution.py:157
  295.2 109.0 %copy-start.1 = (bf16[8192,1,64]{0,2,1:T(8,128)(2,1)S(1)}, bf16[8192,1,64]{0,2,1:T(8,128)(2,1)}, u32[]{:S(2)}) copy-start(bf16[8192,1,64]{0,2,1:T(8,128)(2,1)} %param.18) | copy-start | bytes 3145732
  303.2 99.6 %all-reduce.4.cloned.1.call-start = ((), (), s32[]{:S(2)}) async-start(), calls=%async_computation.2 | async-start | bytes 524288 | tf_op jit(solution)/shard_map/psum | solution.py:162
Sparse Core Ops, SparseCore 0:
  79.8 53.2 all-gather.6
  244.5 8.4 reduce-scatter.1
  303.3 19.0 all-reduce.5
  330.5 72.2 all-reduce.3
where the time goes:
time: 412 us; the launch traced here: 411 us
  blocking collectives  223 us (54%)
  waiting for transfers between devices  100 us (24%)
  matrix products  37.1 us (9%)
  local copies, waits for them, and re-layouts  24.6 us (6%)
  between operations  13.3 us (3%)
  other arithmetic  12.6 us (3%)
    psum x1, waiting for transfers between devices, per_device(): down_total = lax.psum(down_part, 'tp')  72.4 us
    all_gather x2, blocking collectives, joined(): gathered = jax.tree.map(lambda a: lax.all_gather(a, axis), part)  62.7 us
    all_gather x1, blocking collectives, spread_rows(): across = lax.all_gather(shard, 'tp', axis=2, tiled=True)  32.7 us
    all_gather x1, blocking collectives, half_rows_of(): return lax.all_gather(shard, 'tp', axis=2, tiled=True)  30.8 us
    all_gather x1, blocking collectives, per_device(): lax.all_gather(key_part, 'tp', axis=1, tiled=True)  30.6 us
    all_gather x1, blocking collectives, per_device(): lax.all_gather(value_part, 'tp', axis=1, tiled=True)  30.6 us
    all_gather x1, blocking collectives, per_device(): lax.all_gather(query_part, 'tp', axis=1, tiled=True)  30.5 us
    psum x1, waiting for transfers between devices, per_device(): gate_total, up_total = lax.psum((gate_part, up_part), 'sub')  19.1 us
  transfers between devices with their start and end apart: 4, of which 3 were waited for; matrix products, arithmetic and copies ran while one was open for 6% of the time, Pallas kernels for 0%

commit v1 on v0

--- a/solution.py
+++ b/solution.py
@@ -94,7 +94,7 @@
     query, key_new, value_new = (
         lax.all_gather(query_part, "tp", axis=1, tiled=True),
         lax.all_gather(key_part, "tp", axis=1, tiled=True),
-        lax.all_gather(value_part, "tp", axis=1, tiled=True),
+        jnp.concatenate(lax.all_gather(value_part, "tp"), axis=1),
     )
     query_heads = query.shape[1] // HD
     kv_heads = key_new.shape[1] // HD

time: 412 us -> 412 us (level)
  no operation moved by 1% of the time
where the time goes in v1:
time: 412 us; the launch traced here: 411 us
  blocking collectives  223 us (54%)
  waiting for transfers between devices  100 us (24%)
  matrix products  37.1 us (9%)
  local copies, waits for them, and re-layouts  24.6 us (6%)
  between operations  13.3 us (3%)
  other arithmetic  12.6 us (3%)
    psum x1, waiting for transfers between devices, per_device(): down_total = lax.psum(down_part, 'tp')  72.4 us
    all_gather x2, blocking collectives, joined(): gathered = jax.tree.map(lambda a: lax.all_gather(a, axis), part)  62.7 us
    all_gather x1, blocking collectives, spread_rows(): across = lax.all_gather(shard, 'tp', axis=2, tiled=True)  32.7 us
    all_gather x1, blocking collectives, half_rows_of(): return lax.all_gather(shard, 'tp', axis=2, tiled=True)  30.8 us
    all_gather x1, blocking collectives, per_device(): lax.all_gather(key_part, 'tp', axis=1, tiled=True)  30.6 us
    all_gather x1, blocking collectives, per_device(): lax.all_gather(value_part, 'tp')  30.6 us
    all_gather x1, blocking collectives, per_device(): lax.all_gather(query_part, 'tp', axis=1, tiled=True)  30.5 us
    psum x1, waiting for transfers between devices, per_device(): gate_total, up_total = lax.psum((gate_part, up_part), 'sub')  19.1 us
  transfers between devices with their start and end apart: 4, of which 3 were waited for; matrix products, arithmetic and copies ran while one was open for 6% of the time, Pallas kernels for 0%

profile of v1, /device:TPU:0, one launch (start us, length us, event | category | flops | bytes accessed | tf_op | source)
XLA Modules:
  0.0 410.7 jit_solution(5224157179154109241)
XLA Ops:
  6.6 32.7 %all_gather.39 = bf16[16,1,4096]{2,0,1:T(8,128)(2,1)S(1)} all-gather(bf16[16,1,512]{2,0,1:T(8,128)(2,1)} %param.15), channel_id=1, replica_groups=mesh['grp'=2,'tp'=8,'sub'=2] {'tp'}, dimensions={2}, use_global_device_ids=true | all-gather | bytes 147456 | tf_op jit(solution)/shard_map/all_gather | solution.py:39
  39.3 2.0 all_gather.40
  41.3 0.2 fusion.18
  41.5 0.8 mul.250
  42.3 0.1 fusion.24
  42.4 4.6 %fusion.12 = bf16[16,512]{1,0:T(8,128)(2,1)S(1)} fusion(bf16[16,8192]{1,0:T(8,128)(2,1)S(1)} %bitcast.88, bf16[8192,1,512]{2,0,1:T(8,128)(2,1)} %param.17), kind=kOutput, calls=%fused_computation.18 | convolution fusion | flops 134225920 | bytes 8667136 | tf_op jit(solution)/shard_map/dot_general | solution.py:85
  47.0 30.5 %all_gather.41 = bf16[16,4096]{1,0:T(8,128)(2,1)S(1)} all-gather(bf16[16,512]{1,0:T(8,128)(2,1)S(1)} %fusion.12), channel_id=1, replica_groups=mesh['grp'=2,'tp'=8,'sub'=2] {'tp'}, dimensions={1}, use_global_device_ids=true | all-gather | bytes 147456 | tf_op jit(solution)/shard_map/all_gather | solution.py:95
  77.7 0.1 multiply_cosine_fusion
  77.8 0.1 fusion.27
  78.0 0.3 fusion.47
  78.3 1.3 fusion.25
  79.7 0.2 fusion.26
  79.9 31.0 %all-gather.1 = f32[128,4,8]{2,1,0:T(4,128)S(1)} all-gather(f32[16,4,8]{2,1,0:T(4,128)S(1)} %fusion.26), channel_id=3, replica_groups=mesh['grp'=2,'tp'=8,'sub'=2] {'tp'}, dimensions={0}, use_global_device_ids=true | all-gather | bytes 18432 | tf_op jit(solution)/shard_map/all_gather | solution.py:14
  110.9 0.1 copy.68
  111.0 0.1 copy.66
  111.1 31.7 %all-gather = f32[128,4,8]{2,1,0:T(4,128)S(1)} all-gather(f32[16,4,8]{2,1,0:T(4,128)S(1)} %get-tuple-element.236), channel_id=2, replica_groups=mesh['grp'=2,'tp'=8,'sub'=2] {'tp'}, dimensions={0}, use_global_device_ids=true | all-gather | bytes 18432 | tf_op jit(solution)/shard_map/all_gather | solution.py:14
  142.8 0.1 copy.67
  142.9 0.1 copy.65
  143.0 0.4 fusion.15
  143.4 30.6 %all-gather.4 = bf16[8,64,16]{1,2,0:T(8,128)(2,1)S(1)} all-gather(bf16[1,64,16]{1,2,0:T(8,128)(2,1)S(1)} %fusion.15), channel_id=1, replica_groups=mesh['grp'=2,'tp'=8,'sub'=2] {'tp'}, dimensions={0}, use_global_device_ids=true | all-gather | bytes 18432 | tf_op jit(solution)/shard_map/all_gather | solution.py:96
  174.2 0.1 subtract_convert_fusion.1
  174.3 0.3 multiply_reduce_fusion
  174.7 0.4 convolution_convert_fusion
  175.1 30.6 %all-gather.3 = bf16[128,64]{1,0:T(8,128)(2,1)S(1)} all-gather(bf16[16,64]{1,0:T(8,128)(2,1)S(1)} %convolution_convert_fusion), channel_id=5, replica_groups=mesh['grp'=2,'tp'=8,'sub'=2] {'tp'}, dimensions={0}, use_global_device_ids=true | all-gather | bytes 18432 | tf_op jit(solution)/shard_map/all_gather | solution.py:97
  205.8 9.3 %copy.83 = bf16[512,8,2,512]{3,1,2,0:T(8,128)(2,1)} copy(bf16[512,8,2,512]{3,2,1,0:T(2,128)(2,1)} %bitcast.87) | data formatting | bytes 16777216
  215.1 11.4 %copy.75 = bf16[1024,4096]{1,0:T(8,128)(2,1)} copy(bf16[1024,4096]{0,1:T(8,128)(2,1)} %bitcast.86) | data formatting | bytes 16777216 | tf_op jit(solution)/shard_map/dot_general | solution.py:139
  226.5 1.0 slice.26
  227.5 10.0 %while.19 = (s32[]{:T(128)}, f32[16,4,8]{0,2,1:T(8,128)S(1)}, f32[16,4,8]{0,2,1:T(8,128)S(1)}, f32[16,4,8,128]{3,2,1,0:T(8,128)S(1)}, f32[8,16,4,8]{1,3,2,0:T(8,...) while((s32[]{:T(128)}, f32[16,4,8]{0,2,1:T(8,128)S(1)}, ...), condition=%wide.region_4.5_spmd, body=%wide.region_3.4_spmd.sunk | while | flops 199685 | bytes 815255 | solution.py:19
  227.7 1.2 fusion.57
  229.1 1.2 fusion.57
  230.5 1.2 fusion.57
  231.9 1.2 fusion.57
  233.4 1.2 fusion.57
  234.8 1.2 fusion.57
  236.2 1.2 fusion.57
  237.7 0.3 divide_convert_fusion
  238.1 6.3 %fusion.48 = f32[16,2,512]{2,0,1:T(8,128)} fusion(bf16[16,4096,1]{1,0,2:T(8,128)(2,1)S(1)} %reshape.205, bf16[2,512,4096]{2,1,0:T(8,128)(2,1)} %bitcast.85), kind=kOutput, calls=%fused_computation.77 | convolution fusion | flops 134217728 | bytes 8585216 | tf_op jit(solution)/shard_map/dot_general | solution.py:139
  244.5 8.5 %reduce-scatter.2.cloned.1.call-done = f32[16,1,512]{2,0,1:T(8,128)} async-done(((f32[16,2,512]{2,0,1:T(8,128)}), f32[16,1,512]{2,0,1:T(8,128)}) %reduce-scatter.2.cloned.1.call-update) | async-done | bytes 32784 | tf_op jit(solution)/shard_map/reduce_scatter | solution.py:143
  253.0 0.8 add_convert_fusion.1
  253.8 30.8 %all_gather.51 = bf16[16,1,4096]{2,0,1:T(8,128)(2,1)S(1)} all-gather(bf16[16,1,512]{2,0,1:T(8,128)(2,1)S(1)} %add_convert_fusion.1), channel_id=1, replica_groups=mesh['grp'=2,'tp'=8,'sub'=2] {'tp'}, dimensions={2}, use_global_device_ids=true | all-gather | bytes 147456 | tf_op jit(solution)/shard_map/all_gather | solution.py:44
  284.5 0.1 fusion.21
  284.7 2.6 psum.28
  287.3 7.9 %fusion.7 = f32[16,1792]{1,0:T(8,128)} fusion(bf16[1,4096,1792]{2,1,0:T(8,128)(2,1)} %param.22, bf16[16,1,4096]{2,0,1:T(8,128)(2,1)S(1)} %all_gather.51, f32[4096]{0:T(1024)S(1)} %dynamic_slice.50, f32[16]{0:T(128)S(1)} %add_rsqrt_fusion), kind=kOutput, calls=%fused_computation.12 | convolution fusion | flops 235143168 | bytes 14942272 | tf_op jit(solution)/shard_map/dot_general | solution.py:153
  295.2 7.9 %fusion.5 = f32[16,1792]{1,0:T(8,128)} fusion(bf16[1,4096,1792]{2,1,0:T(8,128)(2,1)} %param.23, bf16[16,1,4096]{2,0,1:T(8,128)(2,1)S(1)} %all_gather.51, f32[4096]{0:T(1024)S(1)} %dynamic_slice.50, f32[16]{0:T(128)S(1)} %add_rsqrt_fusion), kind=kOutput, calls=%fused_computation.10 | convolution fusion | flops 235143168 | bytes 14942272 | tf_op jit(solution)/shard_map/dot_general | solution.py:156
  303.2 19.1 %all-reduce.6.cloned.1.call-done = (f32[16,1792]{1,0:T(8,128)}, f32[16,1792]{1,0:T(8,128)}) async-done(((f32[16,1792]{1,0:T(8,128)}, f32[16,1792]{1,0:T(8,128)}), (f32[16,1792]{1,0:T(8,128)}, f32[16,1792]{1,0:T(8,128)})) %all-reduce.6.cloned.1.call-update) | async-done | bytes 229392 | tf_op jit(solution)/shard_map/psum | solution.py:157
  322.4 8.0 %fusion.3 = f32[16,4096]{1,0:T(8,128)} fusion(bf16[1792,1,4096]{2,0,1:T(8,128)(2,1)} %param.24, f32[16,1792]{1,0:T(8,128)} %get-tuple-element.221, f32[16,1792]{1,0:T(8,128)} %get-tuple-element.222), kind=kOutput, calls=%fused_computation.8 | convolution fusion | flops 235053056 | bytes 15171584 | tf_op jit(solution)/shard_map/dot_general | solution.py:159
  330.4 72.4 %all-reduce.4.cloned.1.call-done = f32[16,4096]{1,0:T(8,128)} async-done(((f32[16,4096]{1,0:T(8,128)}), f32[16,4096]{1,0:T(8,128)}) %all-reduce.4.cloned.1.call-update) | async-done | bytes 262160 | tf_op jit(solution)/shard_map/psum | solution.py:162
  402.8 1.4 fusion.36
  (70 shorter events, 2.4 us)
Async XLA Ops:
  6.5 136.5 %copy-start = (bf16[8192,1,64]{0,2,1:T(8,128)(2,1)S(1)}, bf16[8192,1,64]{0,2,1:T(8,128)(2,1)}, u32[]{:S(2)}) copy-start(bf16[8192,1,64]{0,2,1:T(8,128)(2,1)} %param.18) | copy-start | bytes 3145732
  6.5 71.1 %copy-start.7 = (s32[16]{0:T(128)S(1)}, s32[16]{0:T(128)}, u32[]{:S(2)}) copy-start(s32[16]{0:T(128)} %param.27) | copy-start | bytes 196
  6.5 71.4 %copy-start.3 = (bf16[16,8,4,128]{3,2,1,0:T(4,128)(2,1)S(1)}, bf16[16,8,4,128]{3,2,1,0:T(4,128)(2,1)}, u32[]{:S(2)}) copy-start(bf16[16,8,4,128]{3,2,1,0:T(4,128)(2,1)} %param.25) | copy-start | bytes 393220
  6.5 71.8 %copy-start.4 = (bf16[16,8,4,128]{3,2,1,0:T(4,128)(2,1)S(1)}, bf16[16,8,4,128]{3,2,1,0:T(4,128)(2,1)}, u32[]{:S(2)}) copy-start(bf16[16,8,4,128]{3,2,1,0:T(4,128)(2,1)} %param.26) | copy-start | bytes 393220
  6.5 168.1 %copy-start.2 = (bf16[8192,1,64]{0,2,1:T(8,128)(2,1)S(1)}, bf16[8192,1,64]{0,2,1:T(8,128)(2,1)}, u32[]{:S(2)}) copy-start(bf16[8192,1,64]{0,2,1:T(8,128)(2,1)} %param.19) | copy-start | bytes 3145732
  6.5 219.9 %all-gather.7.cloned.1.call-start = ((), (), s32[]{:S(2)}) async-start(), calls=%async_computation.3 | async-start | bytes 2359296 | tf_op jit(solution)/shard_map/all_gather | solution.py:14
  79.7 173.3 %reduce-scatter.2.cloned.1.call-start = ((), (), s32[]{:S(2)}) async-start(), calls=%async_computation.1 | async-start | bytes 98304 | tf_op jit(solution)/shard_map/reduce_scatter | solution.py:143
  215.1 29.3 %copy-start.6 = (f32[8192]{0:T(1024)S(1)}, f32[8192]{0:T(1024)}, u32[]{:S(2)}) copy-start(f32[8192]{0:T(1024)} %param.21) | copy-start | bytes 98308
  215.1 37.9 %copy-start.5 = (bf16[16,1,512]{2,0,1:T(8,128)(2,1)S(1)}, bf16[16,1,512]{2,0,1:T(8,128)(2,1)}, u32[]{:S(2)}) copy-start(bf16[16,1,512]{2,0,1:T(8,128)(2,1)} %param.15) | copy-start | bytes 49156
  244.4 78.0 %all-reduce.6.cloned.1.call-start = ((), (), s32[]{:S(2)}) async-start(), calls=%async_computation.4 | async-start | bytes 458752 | tf_op jit(solution)/shard_map/psum | solution.py:157
  295.2 109.0 %copy-start.1 = (bf16[8192,1,64]{0,2,1:T(8,128)(2,1)S(1)}, bf16[8192,1,64]{0,2,1:T(8,128)(2,1)}, u32[]{:S(2)}) copy-start(bf16[8192,1,64]{0,2,1:T(8,128)(2,1)} %param.18) | copy-start | bytes 3145732
  303.2 99.6 %all-reduce.4.cloned.1.call-start = ((), (), s32[]{:S(2)}) async-start(), calls=%async_computation.2 | async-start | bytes 524288 | tf_op jit(solution)/shard_map/psum | solution.py:162
Sparse Core Ops, SparseCore 0:
  79.8 53.2 all-gather.6
  244.5 8.4 reduce-scatter.1
  303.3 19.0 all-reduce.5
  330.5 72.2 all-reduce.3
